TPU v7x, 128 devices: a whole 4x4x4 slice. The times are simulated.
128 devices in a mesh: batch: 1, row: 16 (over z, y), col: 8 (over x, core).
Axes of the slice: x: 4, y: 4, z: 4, core: 2. Of those that a mesh axis runs over, the one named last changes fastest.
Arguments:
- l_mat: bfloat16 [1024, 1024], P(('batch', 'row'), 'col')
- b_mat: bfloat16 [1024, 65536], P(('batch', 'row'), 'col')
Outputs:
- output: bfloat16 [1024, 65536], P(('batch', 'row'), 'col')
All inputs are finite; a program needn't handle non-finite values.
Results may differ from a plain program's by a relative error of at most 0.001.
Values are sent between devices in bfloat16 or wider.
A program may use at most 1 GiB of HBM per device.

v0:
```python
import jax
import jax.numpy as jnp
from jax import lax
from jax.sharding import PartitionSpec as P


def solution(mesh):
    block_spec = P(('batch', 'row'), 'col')

    def local_product(l_block, b_block):
        l_strip = lax.all_gather(l_block, 'col', axis=1, tiled=True)
        b_strip = lax.all_gather(b_block, 'row', axis=0, tiled=True)
        result = jnp.dot(l_strip, b_strip, preferred_element_type=jnp.float32)
        return result.astype(b_block.dtype)

    return jax.shard_map(local_product, mesh=mesh, in_specs=(block_spec, block_spec), out_specs=block_spec, check_vma=False)
```

profile of v0, /device:TPU:32, one launch (start us, length us, event | category | flops | bytes accessed | tf_op | source)
XLA Modules:
  0.0 138.9 jit_solution(16243182225995312985)
XLA Ops:
  6.5 0.0 all-gather.2.cloned.1.call-start
  6.5 0.7 all-gather.2.cloned.1.call-update
  7.3 13.2 %all_gather.6 = bf16[64,1024]{1,0:T(8,128)(2,1)S(1)} all-gather(bf16[64,128]{1,0:T(8,128)(2,1)} %param.2), channel_id=1, replica_groups=mesh['batch'=1,'row'=16,'col'=8] {'col'}, dimensions={1}, use_global_device_ids=true | all-gather | bytes 147456 | tf_op jit(solution)/shard_map/all_gather | solution.py:11
  20.4 101.9 %all-gather.2.cloned.1.call-done = bf16[1024,8192]{1,0:T(8,128)(2,1)} async-done(((bf16[64,8192]{1,0:T(8,128)(2,1)}), bf16[1024,8192]{1,0:T(8,128)(2,1)}) %all-gather.2.cloned.1.call-update) | async-done | bytes 16777232 | tf_op jit(solution)/shard_map/all_gather | solution.py:12
  122.3 9.8 %convolution_convert_fusion = bf16[64,8192]{1,0:T(8,128)(2,1)} fusion(bf16[64,1024]{1,0:T(8,128)(2,1)S(1)} %all_gather.6, bf16[1024,8192]{1,0:T(8,128)(2,1)} %all-gather.2.cloned.1.call-done), kind=kOutput, calls=%fused_computation | convolution fusion | flops 1074266112 | bytes 17956864 | tf_op jit(solution)/shard_map/dot_general | solution.py:13
Async XLA Ops:
  6.5 115.7 %all-gather.2.cloned.1.call-start = ((), (), s32[]{:S(2)}) async-start(), calls=%async_computation | async-start | bytes 17825792 | tf_op jit(solution)/shard_map/all_gather | solution.py:12
Sparse Core Ops, SparseCore 0:
  9.5 112.7 all-gather.1
where the time goes:
time: 140 us; the launch traced here: 139 us
  waiting for transfers between devices  103 us (74%)
  between operations  13.4 us (10%)
  blocking collectives  13.2 us (9%)
  matrix products  9.76 us (7%)
    all_gather x1, waiting for transfers between devices, local_product(): b_strip = lax.all_gather(b_block, 'row', axis=0, tiled=True)  102 us
    all_gather x1, blocking collectives, local_product(): l_strip = lax.all_gather(l_block, 'col', axis=1, tiled=True)  13.2 us
    dot_general x1, matrix products, local_product(): result = jnp.dot(l_strip, b_strip, preferred_element_type=jnp.float32)  9.76 us
  transfers between devices with their start and end apart: 1, of which 1 were waited for; matrix products, arithmetic and copies ran while one was open for 0% of the time, Pallas kernels for 0%

commit v1 on v0

v1 whole, which is shorter than its diff:
```python
import jax
import jax.numpy as jnp
from jax import lax
from jax.experimental import pallas as pl
from jax.experimental.pallas import tpu as pltpu
from jax.sharding import PartitionSpec as P

MESH = pl.DeviceIdType.MESH
RING = 4
PIECES = 2
PLANE = [(dz, dy) for dz in range(RING) for dy in range(RING) if (dz, dy) != (0, 0)]
ORDER = [(1, 1), (3, 3), (1, 3), (3, 1), (2, 1), (2, 3), (1, 2), (3, 2), (2, 2), (0, 1), (0, 3), (1, 0), (3, 0), (0, 2), (2, 0)]


def kernel(l_ref, b_ref, o_ref, b_own, b_all, l_all, x_all, load_sem, b_send, b_recv, x_send, x_recv, l_send, l_recv, s_send, s_recv, f_send, f_recv, out_sem):
    row, col = lax.axis_index('row'), lax.axis_index('col')
    z, y, x, core = row // RING, row % RING, col // 2, col % 2
    rows, width = b_all.shape[2], b_all.shape[3]
    chunk = PIECES * width

    def at(dz, dy):
        return lax.rem(z + dz, RING) * RING + lax.rem(y + dy, RING)

    def cols(r, h):
        return pl.ds(pl.multiple_of(r * chunk + h * width, width), width)

    loads = [pltpu.make_async_copy(b_ref, b_own, load_sem.at[0]),
             pltpu.make_async_copy(l_ref, l_all.at[col, pl.ds(pl.multiple_of(row * rows, rows), rows)], load_sem.at[1])]
    loads += [pltpu.make_async_copy(b_ref.at[:, cols(row, h)], b_all.at[h, row], load_sem.at[2 + h]) for h in range(PIECES)]
    for copy in loads:
        copy.start()

    barrier = pltpu.get_barrier_semaphore()
    for dz, dy in PLANE:
        pl.semaphore_signal(barrier, inc=1, device_id=(0, at(dz, dy), col), device_id_type=MESH)
    for dx in (1, 2, 3):
        pl.semaphore_signal(barrier, inc=1, device_id=(0, row, lax.rem(x + dx, RING) * 2 + core), device_id_type=MESH)
    pl.semaphore_signal(barrier, inc=1, device_id=(0, row, x * 2 + 1 - core), device_id_type=MESH)
    pl.semaphore_wait(barrier, len(PLANE) + 4)
    for copy in loads:
        copy.wait()

    def l_copy(i):
        dz, dy = ORDER[i]
        here = l_all.at[col, pl.ds(pl.multiple_of(row * rows, rows), rows)]
        return pltpu.make_async_remote_copy(src_ref=here, dst_ref=here, send_sem=l_send.at[i], recv_sem=l_recv.at[i],
                                            device_id=(0, at(dz, dy), col), device_id_type=MESH)

    @pl.when(z >= x)
    def _():
        for i in range(len(ORDER)):
            l_copy(i).start()

    def b_copy(h, i):
        peer = at(*ORDER[i])
        return pltpu.make_async_remote_copy(src_ref=b_own.at[:, cols(peer, h)], dst_ref=b_all.at[h, row], send_sem=b_send.at[h, i],
                                            recv_sem=b_recv.at[h, i], device_id=(0, peer, col), device_id_type=MESH)

    for h in range(PIECES):
        for i in range(len(ORDER)):
            b_copy(h, i).start()

    for i, (dz, dy) in enumerate(ORDER):
        @pl.when(lax.rem(z + RING - dz, RING) >= x)
        def _(i=i):
            l_copy(i).wait_recv()

    group = RING * rows

    def span(block, g):
        return l_all.at[block, pl.ds(g * group, group)]

    def s_copy(k, g):
        to = lax.rem(x + k + 1, RING) * 2 + core if k < 3 else x * 2 + 1 - core
        return pltpu.make_async_remote_copy(src_ref=span(col, g), dst_ref=span(col, g), send_sem=s_send.at[k, g], recv_sem=s_recv.at[k, g],
                                            device_id=(0, row, to), device_id_type=MESH)

    def f_copy(k, g):
        block = lax.rem(x + RING - k - 1, RING) * 2 + core
        return pltpu.make_async_remote_copy(src_ref=span(block, g), dst_ref=span(block, g), send_sem=f_send.at[k, g], recv_sem=f_recv.at[k, g],
                                            device_id=(0, row, x * 2 + 1 - core), device_id_type=MESH)

    for g in range(RING):
        @pl.when(g >= x)
        def _(g=g):
            for k in range(4):
                s_copy(k, g).start()
    for g in range(RING):
        for k in range(3):
            @pl.when(g >= lax.rem(x + RING - k - 1, RING))
            def _(k=k, g=g):
                s_copy(k, g).wait_recv()
                f_copy(k, g).start()
    for g in range(RING):
        @pl.when(g >= x)
        def _(g=g):
            s_copy(3, g).wait_recv()
        for k in range(3):
            @pl.when(g >= lax.rem(x + RING - k - 1, RING))
            def _(k=k, g=g):
                f_copy(k, g).wait_recv()

    def x_copy(h, i):
        peer = at(*ORDER[i])
        return pltpu.make_async_remote_copy(src_ref=x_all.at[h, peer], dst_ref=o_ref.at[:, cols(row, h)], send_sem=x_send.at[h, i],
                                            recv_sem=x_recv.at[h, i], device_id=(0, peer, col), device_id_type=MESH)

    outs = []
    for h in range(PIECES):
        for i in range(len(ORDER)):
            b_copy(h, i).wait_recv()
        for g in range(RING):
            depth = (g + 1) * group
            left = jnp.concatenate([l_all[k, g * group:(g + 1) * group, :] for k in range(2 * (g + 1))], axis=1)
            right = b_all[h, :(g + 1) * RING].reshape(depth, width)
            total = jnp.dot(left, right, preferred_element_type=jnp.float32)
            x_all[h, g * RING:(g + 1) * RING] = total.astype(jnp.bfloat16).reshape(RING, rows, width)
        for i in range(len(ORDER)):
            x_copy(h, i).start()
        out = pltpu.make_async_copy(x_all.at[h, row], o_ref.at[:, cols(row, h)], out_sem.at[h])
        out.start()
        outs.append(out)

    for i in range(len(ORDER)):
        @pl.when(z >= x)
        def _(i=i):
            l_copy(i).wait_send()
    for g in range(RING):
        @pl.when(g >= x)
        def _(g=g):
            for k in range(4):
                s_copy(k, g).wait_send()
        for k in range(3):
            @pl.when(g >= lax.rem(x + RING - k - 1, RING))
            def _(k=k, g=g):
                f_copy(k, g).wait_send()
    for h in range(PIECES):
        for i in range(len(ORDER)):
            b_copy(h, i).wait_send()
            x_copy(h, i).wait()
        outs[h].wait()


def solution(mesh):
    block_spec = P(('batch', 'row'), 'col')
    dma = pltpu.SemaphoreType.DMA

    def step(l_block, b_block):
        rows, columns = b_block.shape
        width = columns // 16 // PIECES
        n = len(ORDER)
        return pl.pallas_call(
            kernel,
            out_shape=jax.ShapeDtypeStruct(b_block.shape, b_block.dtype),
            in_specs=[pl.BlockSpec(memory_space=pl.ANY)] * 2,
            out_specs=pl.BlockSpec(memory_space=pl.ANY),
            scratch_shapes=[
                pltpu.VMEM((rows, columns), jnp.bfloat16),
                pltpu.VMEM((PIECES, 16, rows, width), jnp.bfloat16),
                pltpu.VMEM((8, 16 * rows, 128), jnp.bfloat16),
                pltpu.VMEM((PIECES, 16, rows, width), jnp.bfloat16),
                dma((2 + PIECES,)),
                dma((PIECES, n)), dma((PIECES, n)), dma((PIECES, n)), dma((PIECES, n)),
                dma((n,)), dma((n,)),
                dma((4, RING)), dma((4, RING)), dma((3, RING)), dma((3, RING)),
                dma((PIECES,)),
            ],
            compiler_params=pltpu.CompilerParams(collective_id=0, has_side_effects=True),
        )(l_block, b_block)

    return jax.shard_map(step, mesh=mesh, in_specs=(block_spec, block_spec), out_specs=block_spec, check_vma=False)
```

time: 140 us -> 45.1 us (0.32)
  the two profiles are of different devices: /device:TPU:32 before, /device:TPU:28 now
where the time goes in v1:
time: 45.1 us; the launch traced here: 45 us
  Pallas kernels  42.7 us (95%)
  local copies, waits for them, and re-layouts  2.26 us (5%)
    pallas_call x1, Pallas kernels, step(): pl.pallas_call(kernel, out_shape=jax.ShapeDtypeStruct(b_block.shape, b_bl...  42.7 us
    unnamed x1, local copies, waits for them, and re-layouts  2.26 us

profile of v1, /device:TPU:28, one launch (start us, length us, event | category | flops | bytes accessed | tf_op | source)
XLA Modules:
  0.0 45.0 jit_solution(15060377560590149390)
XLA Ops:
  0.0 42.7 %shard_map.28 = bf16[64,8192]{1,0:T(8,128)(2,1)} custom-call(bf16[64,128]{1,0:T(8,128)(2,1)} %l_ref.1, bf16[64,8192]{1,0:T(8,128)(2,1)} %b_ref.1), custom_call_target="tpu_custom_call" | custom-call | tf_op jit(solution)/shard_map/pallas_call | solution.py:152
  42.7 2.3 %copy.4 = bf16[64,8192]{1,0:T(8,128)(2,1)} copy(bf16[64,8192]{1,0:T(8,128)(2,1)} %shard_map.28) | data formatting | bytes 2097152

commit v2 on v0

v2 whole, which is shorter than its diff:
```python
import jax
import jax.numpy as jnp
from jax import lax
from jax.experimental import pallas as pl
from jax.experimental.pallas import tpu as pltpu
from jax.sharding import PartitionSpec as P

MESH = pl.DeviceIdType.MESH
RING = 4
PIECES = 2
SHIFTS = (1, 3, 2, 0)
UP = 1


def kernel(l_ref, b_ref, o_ref, b_own, b_all, l_all, x_all, load_sem, b_send, b_recv, x_send, x_recv, l_send, l_recv, s_send, s_recv, r_send,
           f_send, f_recv, out_sem, ack, ack_x):
    row, col = lax.axis_index('row'), lax.axis_index('col')
    z, y, x, core = row // RING, row % RING, col // 2, col % 2
    rows, width = b_all.shape[2], b_all.shape[3]
    chunk = PIECES * width
    group = RING * rows
    partner = x * 2 + 1 - core

    def cols(r, h):
        return pl.ds(pl.multiple_of(r * chunk + h * width, width), width)

    def there(g, dy):
        return g * RING + lax.rem(y + dy, RING)

    def others(g, act):
        for dy in SHIFTS:
            if dy:
                act(dy)
            else:
                pl.when(z != g)(lambda: act(0))

    here = l_all.at[col, pl.ds(pl.multiple_of(row * rows, rows), rows)]
    loads = [pltpu.make_async_copy(l_ref, here, load_sem.at[0]), pltpu.make_async_copy(b_ref, b_own, load_sem.at[1])]
    loads += [pltpu.make_async_copy(b_ref.at[:, cols(row, h)], b_all.at[h, row], load_sem.at[2 + h]) for h in range(PIECES)]
    for copy in loads:
        copy.start()

    barrier = pltpu.get_barrier_semaphore()

    def greet(sem, to_row, to_col):
        pl.semaphore_signal(sem, inc=1, device_id=(0, to_row, to_col), device_id_type=MESH)

    greet(barrier, row, partner)
    for dy in (1, 2, 3):
        greet(barrier, there(z, dy), col)
    for k in range(1, RING):
        @pl.when(k > x)
        def _(k=k):
            greet(barrier, row, k * 2 + core)
    for g in range(1, RING):
        @pl.when(g > z)
        def _(g=g):
            for dy in range(RING):
                greet(barrier, there(g, dy), col)
    pl.semaphore_wait(barrier, RING + RING * z + x)
    for g in range(RING - 1):
        @pl.when(g < z)
        def _(g=g):
            for dy in range(RING):
                greet(ack.at[z], there(g, dy), col)
    for k in range(RING - 1):
        @pl.when(k < x)
        def _(k=k):
            greet(ack_x.at[x], row, k * 2 + core)
    for copy in loads:
        copy.wait()

    def l_copy(g, dy):
        return pltpu.make_async_remote_copy(src_ref=here, dst_ref=here, send_sem=l_send.at[g, dy], recv_sem=l_recv.at[z, dy],
                                            device_id=(0, there(g, dy), col), device_id_type=MESH)

    def l_from(g, dy):
        return pltpu.make_async_remote_copy(src_ref=here, dst_ref=here, send_sem=l_send.at[g, dy], recv_sem=l_recv.at[g, dy],
                                            device_id=(0, there(g, dy), col), device_id_type=MESH)

    def b_copy(h, g, dy, sender):
        return pltpu.make_async_remote_copy(src_ref=b_own.at[:, cols(there(g, dy), h)], dst_ref=b_all.at[h, row], send_sem=b_send.at[h, g, dy],
                                            recv_sem=b_recv.at[h, sender, dy], device_id=(0, there(g, dy), col), device_id_type=MESH)

    for g in range(RING):
        @pl.when((g <= z) & (z >= x))
        def _(g=g):
            others(g, lambda dy: l_copy(g, dy).start())
    for g in range(RING):
        @pl.when(g > z)
        def _(g=g):
            pl.semaphore_wait(ack.at[g], RING)

            @pl.when(z >= x)
            def _():
                others(g, lambda dy: l_copy(g, dy).start())
    for h in range(PIECES):
        for g in range(RING):
            others(g, lambda dy, g=g, h=h: b_copy(h, g, dy, z).start())

    def span(block, g):
        return l_all.at[block, pl.ds(g * group, group)]

    def source(k):
        return lax.rem(x + RING - k - 1, RING)

    def s_copy(k, g):
        to = lax.rem(x + k + 1, RING) * 2 + core if k < 3 else partner
        return pltpu.make_async_remote_copy(src_ref=span(col, g), dst_ref=span(col, g), send_sem=s_send.at[k, g], recv_sem=s_recv.at[k, g],
                                            device_id=(0, row, to), device_id_type=MESH)

    def r_copy(k, g):
        part = span(source(k) * 2 + core, g)
        to = lax.rem(x + (1 if k == 0 else 3), RING) * 2 + core
        return pltpu.make_async_remote_copy(src_ref=part, dst_ref=part, send_sem=r_send.at[k, g], recv_sem=s_recv.at[1, g],
                                            device_id=(0, row, to), device_id_type=MESH)

    def f_copy(k, g):
        part = span(source(k) * 2 + core, g)
        return pltpu.make_async_remote_copy(src_ref=part, dst_ref=part, send_sem=f_send.at[k, g], recv_sem=f_recv.at[k, g],
                                            device_id=(0, row, partner), device_id_type=MESH)

    def relays(k, g):
        upward = (source(k) == 1) | (source(k) == 2) | ((source(k) == 0) & (g == UP))
        return (g >= source(k)) & (upward if k == 0 else jnp.logical_not(upward))

    for k in range(1, RING):
        @pl.when(k > x)
        def _(k=k):
            pl.semaphore_wait(ack_x.at[k], 1)
    for g in range(RING):
        @pl.when(g >= x)
        def _(g=g):
            others(g, lambda dy: l_from(g, dy).wait_recv())
            for k in (0, 2, 3):
                s_copy(k, g).start()

    def near(g):
        for k in (0, 2):
            @pl.when(g >= source(k))
            def _(k=k):
                s_copy(k, g).wait_recv()

                @pl.when(relays(k, g))
                def _():
                    r_copy(k, g).start()
                f_copy(k, g).start()

    def far(g):
        @pl.when(g >= source(1))
        def _():
            s_copy(1, g).wait_recv()
            f_copy(1, g).start()

    def across(g):
        @pl.when(g >= x)
        def _():
            s_copy(3, g).wait_recv()
        for k in range(3):
            @pl.when(g >= source(k))
            def _(k=k):
                f_copy(k, g).wait_recv()

    def x_copy(h, g, dy, sender):
        return pltpu.make_async_remote_copy(src_ref=x_all.at[h, there(g, dy)], dst_ref=o_ref.at[:, cols(row, h)], send_sem=x_send.at[h, g, dy],
                                            recv_sem=x_recv.at[h, sender, dy], device_id=(0, there(g, dy), col), device_id_type=MESH)

    def out_copy(h):
        return pltpu.make_async_copy(x_all.at[h, row], o_ref.at[:, cols(row, h)], out_sem.at[h])

    def finish(h, g):
        others(g, lambda dy: b_copy(h, g, dy, g).wait_recv())
        depth = (g + 1) * group
        left = jnp.concatenate([l_all[k, g * group:(g + 1) * group, :] for k in range(2 * (g + 1))], axis=1)
        right = b_all[h, :(g + 1) * RING].reshape(depth, width)
        total = jnp.dot(left, right, preferred_element_type=jnp.float32)
        x_all[h, g * RING:(g + 1) * RING] = total.astype(jnp.bfloat16).reshape(RING, rows, width)
        others(g, lambda dy: x_copy(h, g, dy, z).start())
        pl.when(z == g)(lambda: out_copy(h).start())

    for g in range(RING):
        near(g)
    far(0)
    for g in range(RING):
        if g + 1 < RING:
            far(g + 1)
        across(g)
        finish(0, g)
    for h in range(1, PIECES):
        for g in range(RING):
            finish(h, g)

    for g in range(RING):
        @pl.when(z >= x)
        def _(g=g):
            others(g, lambda dy: l_copy(g, dy).wait_send())

        @pl.when(g >= x)
        def _(g=g):
            for k in (0, 2, 3):
                s_copy(k, g).wait_send()
        for k in range(3):
            @pl.when(g >= source(k))
            def _(k=k, g=g):
                f_copy(k, g).wait_send()
        for k in (0, 2):
            @pl.when(relays(k, g))
            def _(k=k, g=g):
                r_copy(k, g).wait_send()
    for h in range(PIECES):
        for g in range(RING):
            others(g, lambda dy, g=g, h=h: b_copy(h, g, dy, z).wait_send())
            others(g, lambda dy, g=g, h=h: x_copy(h, g, dy, z).wait_send())
    for h in range(PIECES):
        for g in range(RING):
            others(g, lambda dy, g=g, h=h: x_copy(h, g, dy, g).wait_recv())
        out_copy(h).wait()


def solution(mesh):
    block_spec = P(('batch', 'row'), 'col')
    dma, vmem = pltpu.SemaphoreType.DMA, pltpu.VMEM

    def step(l_block, b_block):
        rows, columns = b_block.shape
        width = columns // 16 // PIECES
        pair = [dma((PIECES, RING, RING))] * 2
        return pl.pallas_call(
            kernel,
            out_shape=jax.ShapeDtypeStruct(b_block.shape, b_block.dtype),
            in_specs=[pl.BlockSpec(memory_space=pl.ANY)] * 2,
            out_specs=pl.BlockSpec(memory_space=pl.ANY),
            scratch_shapes=[
                vmem((rows, columns), jnp.bfloat16),
                vmem((PIECES, 16, rows, width), jnp.bfloat16),
                vmem((8, 16 * rows, 128), jnp.bfloat16),
                vmem((PIECES, 16, rows, width), jnp.bfloat16),
                dma((2 + PIECES,)), *pair, *pair,
                dma((RING, RING)), dma((RING, RING)),
                dma((4, RING)), dma((4, RING)), dma((3, RING)), dma((3, RING)), dma((3, RING)),
                dma((PIECES,)), pltpu.SemaphoreType.REGULAR((RING,)), pltpu.SemaphoreType.REGULAR((RING,)),
            ],
            compiler_params=pltpu.CompilerParams(collective_id=0, has_side_effects=True),
        )(l_block, b_block)

    return jax.shard_map(step, mesh=mesh, in_specs=(block_spec, block_spec), out_specs=block_spec, check_vma=False)
```

time: 140 us -> 40.8 us (0.29)
  the two profiles are of different devices: /device:TPU:32 before, /device:TPU:31 now
where the time goes in v2:
time: 40.8 us; the launch traced here: 40.6 us
  Pallas kernels  38.3 us (94%)
  local copies, waits for them, and re-layouts  2.26 us (6%)
    pallas_call x1, Pallas kernels, step(): pl.pallas_call(kernel, out_shape=jax.ShapeDtypeStruct(b_block.shape, b_bl...  38.3 us
    unnamed x1, local copies, waits for them, and re-layouts  2.26 us

profile of v2, /device:TPU:31, one launch (start us, length us, event | category | flops | bytes accessed | tf_op | source)
XLA Modules:
  0.0 40.6 jit_solution(14621025880264948449)
XLA Ops:
  0.0 38.3 %shard_map.28 = bf16[64,8192]{1,0:T(8,128)(2,1)} custom-call(bf16[64,128]{1,0:T(8,128)(2,1)} %l_ref.1, bf16[64,8192]{1,0:T(8,128)(2,1)} %b_ref.1), custom_call_target="tpu_custom_call" | custom-call | tf_op jit(solution)/shard_map/pallas_call | solution.py:228
  38.4 2.3 %copy.4 = bf16[64,8192]{1,0:T(8,128)(2,1)} copy(bf16[64,8192]{1,0:T(8,128)(2,1)} %shard_map.28) | data formatting | bytes 2097152

commit v3 on v0

v3 whole, which is shorter than its diff:
```python
import jax
import jax.numpy as jnp
from jax import lax
from jax.experimental import pallas as pl
from jax.experimental.pallas import tpu as pltpu
from jax.sharding import PartitionSpec as P

MESH = pl.DeviceIdType.MESH
RING = 4
PIECES = 2
LINES = (0, 1, 2, 3)
SHIFTS = (1, 3, 2, 0)
UP = 1


def kernel(l_ref, b_ref, o_ref, b_own, b_all, l_all, x_all, load_sem, b_send, b_recv, x_send, x_recv, l_send, l_recv, s_send, s_recv, c_send,
           c_recv, ack, ack_x, ack_core):
    row, col = lax.axis_index('row'), lax.axis_index('col')
    z, y, x, core = row // RING, row % RING, col // 2, col % 2
    rows, width = b_all.shape[2], b_all.shape[3]
    chunk = PIECES * width
    group = RING * rows
    partner = x * 2 + 1 - core

    def cols(r, h):
        return pl.ds(pl.multiple_of(r * chunk + h * width, width), width)

    def there(g, dy):
        return g * RING + lax.rem(y + dy, RING)

    def others(g, act):
        for dy in SHIFTS:
            if dy:
                act(dy)
            else:
                pl.when(z != g)(lambda: act(0))

    def line(k, act):
        for dy in SHIFTS:
            if k or dy:
                act(dy)

    here = l_all.at[col, pl.ds(pl.multiple_of(row * rows, rows), rows)]
    loads = [pltpu.make_async_copy(l_ref, here, load_sem.at[0]), pltpu.make_async_copy(b_ref, b_own, load_sem.at[1])]
    for copy in loads:
        copy.start()
    for h in range(PIECES):
        pltpu.make_async_copy(b_ref.at[:, cols(row, h)], b_all.at[h, row], load_sem.at[2]).start()
    loads.append(pltpu.make_async_copy(b_all.at[:, row], b_all.at[:, row], load_sem.at[2]))

    barrier = pltpu.get_barrier_semaphore()

    def greet(sem, to_row, to_col):
        pl.semaphore_signal(sem, inc=1, device_id=(0, to_row, to_col), device_id_type=MESH)

    pl.when(core == 1)(lambda: greet(barrier, row, partner))
    for r in range(1, RING * RING):
        pl.when(r > row)(lambda r=r: greet(barrier, r, col))
    for k in range(1, RING):
        pl.when(k > x)(lambda k=k: greet(barrier, row, k * 2 + core))
    pl.when(row + x + 1 - core > 0)(lambda: pl.semaphore_wait(barrier, row + x + 1 - core))
    for r in range(RING * RING - 1):
        pl.when(r < row)(lambda r=r: greet(ack.at[z], r, col))
    for k in range(RING - 1):
        pl.when(k < x)(lambda k=k: greet(ack_x.at[x], row, k * 2 + core))
    pl.when(core == 0)(lambda: greet(ack_core, row, partner))
    for copy in loads:
        copy.wait()

    def l_copy(g, dy):
        return pltpu.make_async_remote_copy(src_ref=here, dst_ref=here, send_sem=l_send, recv_sem=l_recv.at[z],
                                            device_id=(0, there(g, dy), col), device_id_type=MESH)

    def b_copy(h, g, dy):
        return pltpu.make_async_remote_copy(src_ref=b_own.at[:, cols(there(g, dy), h)], dst_ref=b_all.at[h, row], send_sem=b_send,
                                            recv_sem=b_recv.at[h, z], device_id=(0, there(g, dy), col), device_id_type=MESH)

    def took(ref, sem):
        pltpu.make_async_copy(ref, ref, sem).wait()

    def from_line(g, whole, less, sem):
        pl.when(z != g)(lambda: took(whole, sem))
        pl.when(z == g)(lambda: took(less, sem))

    def spread(g):
        pl.when(z >= x)(lambda: others(g, lambda dy: l_copy(g, dy).start()))

    for g in range(RING):
        pl.when(g < z)(lambda g=g: spread(g))
    for g in range(RING):
        @pl.when(g == z)
        def _(g=g):
            pl.when(y < RING - 1)(lambda: pl.semaphore_wait(ack.at[g], RING - 1 - y))
            spread(g)

        @pl.when(g > z)
        def _(g=g):
            pl.semaphore_wait(ack.at[g], RING)
            spread(g)
    for h in range(PIECES):
        for k in LINES:
            g = lax.rem(z + k, RING)
            line(k, lambda dy, g=g, h=h: b_copy(h, g, dy).start())

    def part(block, g):
        return l_all.at[block, pl.ds(g * group, group)]

    def source(k):
        return lax.rem(x + RING - k - 1, RING)

    def move(block, g, send_sem, recv_sem, to):
        return pltpu.make_async_remote_copy(src_ref=part(block, g), dst_ref=part(block, g), send_sem=send_sem, recv_sem=recv_sem,
                                            device_id=(0, row, to), device_id_type=MESH)

    def s_copy(k, g):
        return move(col, g, s_send, s_recv.at[k, g], lax.rem(x + k + 1, RING) * 2 + core)

    def r_copy(k, g):
        return move(source(k) * 2 + core, g, s_send, s_recv.at[1, g], lax.rem(x + (1 if k == 0 else 3), RING) * 2 + core)

    def c_copy(block, g):
        return move(block, g, c_send, c_recv.at[g], partner)

    def relays(k, g):
        upward = (source(k) == 1) | (source(k) == 2) | ((source(k) == 0) & (g == UP))
        return (g >= source(k)) & (upward if k == 0 else jnp.logical_not(upward))

    def first(g):
        @pl.when(g >= x)
        def _():
            from_line(g, l_all.at[0, pl.ds(0, group)], l_all.at[0, pl.ds(0, group - rows)], l_recv.at[g])
            s_copy(0, g).start()
            s_copy(2, g).start()
            c_copy(col, g).start()

    def near(g):
        for k in (0, 2):
            @pl.when(g >= source(k))
            def _(k=k):
                s_copy(k, g).wait_recv()
                pl.when(relays(k, g))(lambda: r_copy(k, g).start())
                c_copy(source(k) * 2 + core, g).start()

    def far(g):
        @pl.when(g >= source(1))
        def _():
            s_copy(1, g).wait_recv()
            c_copy(source(1) * 2 + core, g).start()

    def across(g):
        took(l_all.at[pl.ds(0, g + 1), pl.ds(0, group)], c_recv.at[g])

    for k in range(1, RING):
        pl.when(k > x)(lambda k=k: pl.semaphore_wait(ack_x.at[k], 1))
    pl.when(core == 1)(lambda: pl.semaphore_wait(ack_core, 1))
    for g in range(RING):
        first(g)
    for g in range(RING):
        near(g)

    def x_copy(h, g, dy):
        return pltpu.make_async_remote_copy(src_ref=x_all.at[h, there(g, dy)], dst_ref=o_ref.at[:, cols(row, h)], send_sem=x_send,
                                            recv_sem=x_recv, device_id=(0, there(g, dy), col), device_id_type=MESH)

    def finish(h, g):
        from_line(g, b_all.at[h, pl.ds(0, RING)], b_all.at[h, pl.ds(0, RING - 1)], b_recv.at[h, g])
        depth = (g + 1) * group
        left = jnp.concatenate([l_all[k, g * group:(g + 1) * group, :] for k in range(2 * (g + 1))], axis=1)
        right = b_all[h, :(g + 1) * RING].reshape(depth, width)
        total = jnp.dot(left, right, preferred_element_type=jnp.float32)
        x_all[h, g * RING:(g + 1) * RING] = total.astype(jnp.bfloat16).reshape(RING, rows, width)
        others(g, lambda dy: x_copy(h, g, dy).start())

    far(0)
    for g in range(RING):
        if g + 1 < RING:
            far(g + 1)
        across(g)
        finish(0, g)
    for h in range(1, PIECES):
        for g in range(RING):
            finish(h, g)
    for h in range(PIECES):
        o_ref[:, cols(row, h)] = x_all[h, row]

    pl.when(z >= x)(lambda: took(l_all.at[0, pl.ds(0, 15 * rows)], l_send))
    pl.when(x % 2 == 0)(lambda: took(l_all.at[:, pl.ds(0, group)], s_send))
    pl.when(x % 2 == 1)(lambda: took(l_all.at[pl.ds(0, 7), pl.ds(0, group)], s_send))
    took(l_all.at[pl.ds(0, 5), pl.ds(0, 2 * group)], c_send)
    took(b_all.at[:, pl.ds(0, 15)], b_send)
    took(b_all.at[:, pl.ds(0, 15)], x_send)
    took(b_all.at[:, pl.ds(0, 15)], x_recv)


def solution(mesh):
    block_spec = P(('batch', 'row'), 'col')
    dma, vmem, plain = pltpu.SemaphoreType.DMA, pltpu.VMEM, pltpu.SemaphoreType.REGULAR

    def step(l_block, b_block):
        rows, columns = b_block.shape
        width = columns // 16 // PIECES
        return pl.pallas_call(
            kernel,
            out_shape=pltpu.VMEM(b_block.shape, b_block.dtype),
            in_specs=[pl.BlockSpec(memory_space=pl.ANY)] * 2,
            out_specs=pl.BlockSpec(memory_space=pltpu.VMEM),
            scratch_shapes=[
                vmem((rows, columns), jnp.bfloat16),
                vmem((PIECES, 16, rows, width), jnp.bfloat16),
                vmem((8, 16 * rows, 128), jnp.bfloat16),
                vmem((PIECES, 16, rows, width), jnp.bfloat16),
                dma((3,)), dma(()), dma((PIECES, RING)), dma(()), dma(()), dma(()), dma((RING,)),
                dma(()), dma((3, RING)), dma(()), dma((RING,)), plain((RING,)), plain((RING,)), plain(()),
            ],
            compiler_params=pltpu.CompilerParams(collective_id=0, has_side_effects=True),
        )(l_block, b_block)

    return jax.shard_map(step, mesh=mesh, in_specs=(block_spec, block_spec), out_specs=block_spec, check_vma=False)
```

time: 140 us -> 39 us (0.28)
  the two profiles are of different devices: /device:TPU:32 before, /device:TPU:25 now
where the time goes in v3:
time: 39 us; the launch traced here: 38.9 us
  Pallas kernels  37.9 us (97%)
  local copies, waits for them, and re-layouts  0.97 us (2%)
    pallas_call x1, Pallas kernels, step(): pl.pallas_call(kernel, out_shape=pltpu.VMEM(b_block.shape, b_block.dtype)...  37.9 us
    unnamed x1, local copies, waits for them, and re-layouts  0.97 us

profile of v3, /device:TPU:25, one launch (start us, length us, event | category | flops | bytes accessed | tf_op | source)
XLA Modules:
  0.0 38.9 jit_solution(12203861693673465160)
XLA Ops:
  0.0 37.9 %shard_map.28 = bf16[64,8192]{1,0:T(8,128)(2,1)S(1)} custom-call(bf16[64,128]{1,0:T(8,128)(2,1)} %l_ref.1, bf16[64,8192]{1,0:T(8,128)(2,1)} %b_ref.1), custom_call_target="tpu_custom_call" | custom-call | tf_op jit(solution)/shard_map/pallas_call | solution.py:202
  37.9 1.0 %copy.4 = bf16[64,8192]{1,0:T(8,128)(2,1)} copy(bf16[64,8192]{1,0:T(8,128)(2,1)S(1)} %shard_map.28) | data formatting | bytes 2097152

commit v4 on v0

v4 whole, which is shorter than its diff:
```python
import jax
import jax.numpy as jnp
from jax import lax
from jax.experimental import pallas as pl
from jax.experimental.pallas import tpu as pltpu
from jax.sharding import PartitionSpec as P

MESH = pl.DeviceIdType.MESH
RING = 4
PARTS = ((0, 256), (256, 256))
SEQUENCE = (
    ('first', 0),
    ('first', 1),
    ('first', 2),
    ('near', 0),
    ('first', 3),
    ('near', 1),
    ('far', 0),
    ('near', 2),
    ('across', 0),
    ('finish', 0, 0),
    ('far', 1),
    ('near', 3),
    ('across', 1),
    ('finish', 0, 1),
    ('far', 2),
    ('across', 2),
    ('finish', 0, 2),
    ('finish', 1, 0),
    ('far', 3),
    ('across', 3),
    ('finish', 0, 3),
    ('finish', 1, 1),
    ('finish', 1, 2),
    ('finish', 1, 3),
)
B_FIRST = ((0, 0), (1, 0))
B_ORDER = ((0, 1), (0, 2), (0, 3), (1, 1), (1, 2), (1, 3))
B_SHIFTS = (1, 3, 2, 0)
X_SHIFTS = (2, 1, 3, 0)
L_SHIFTS = (1, 3, 2, 0)
ITEMS = {
    (0, 0): (0, 0),
    (1, 0): (1, 1),
    (2, 0): (0, 0),
    (3, 0): (0, 0),
    (1, 1): (1, 1),
    (2, 1): (1, 1),
    (3, 1): (1, 1),
    (2, 2): (1, 1),
    (3, 2): (1, 1),
    (3, 3): (0, 0),
}


def kernel(l_ref, b_ref, o_ref, b_own, b_all, l_all, x_all, load_sem, b_send, b_recv, x_send, x_recv, l_send, l_recv, s_send,
           s_recv, c_send, c_recv, ack, ack_x, ack_core):
    row, col = lax.axis_index('row'), lax.axis_index('col')
    z, y, x, core = row // RING, row % RING, col // 2, col % 2
    rows, chunk = b_all.shape[1], b_all.shape[2]
    group = RING * rows
    partner = x * 2 + 1 - core

    def cols(r, h):
        return pl.ds(pl.multiple_of(r * chunk + PARTS[h][0], 128), PARTS[h][1])

    def within(h):
        return pl.ds(*PARTS[h])

    def whole(r):
        return pl.ds(pl.multiple_of(r * chunk, chunk), chunk)

    def there(g, dy):
        return g * RING + lax.rem(y + dy, RING)

    def others(g, act, shifts):
        for dy in shifts:
            if dy:
                act(dy)
            else:
                pl.when(z != g)(lambda: act(0))

    def piece(block):
        return l_all.at[block, pl.ds(pl.multiple_of(row * rows, rows), rows)]

    loads = [pltpu.make_async_copy(l_ref, piece(col), load_sem.at[0]), pltpu.make_async_copy(b_ref, b_own, load_sem.at[1]),
             pltpu.make_async_copy(b_ref.at[:, whole(row)], b_all.at[row], load_sem.at[2])]
    for copy in loads:
        copy.start()

    barrier = pltpu.get_barrier_semaphore()

    def greet(sem, to_row, to_col):
        pl.semaphore_signal(sem, inc=1, device_id=(0, to_row, to_col), device_id_type=MESH)

    pl.when(core == 1)(lambda: greet(barrier, row, partner))
    for r in range(1, RING * RING):
        pl.when(r > row)(lambda r=r: greet(barrier, r, col))
    for k in range(1, RING):
        pl.when(k > x)(lambda k=k: greet(barrier, row, k * 2 + core))
    pl.when(row + x + 1 - core > 0)(lambda: pl.semaphore_wait(barrier, row + x + 1 - core))
    for r in range(RING * RING - 1):
        pl.when(r < row)(lambda r=r: greet(ack.at[z], r, col))
    for k in range(RING - 1):
        pl.when(k < x)(lambda k=k: greet(ack_x.at[x], row, k * 2 + core))
    pl.when(core == 0)(lambda: greet(ack_core, row, partner))
    loads[0].wait()

    def took(ref, sem):
        pltpu.make_async_copy(ref, ref, sem).wait()

    def from_line(g, four, three, sem):
        pl.when(z != g)(lambda: took(four, sem))
        pl.when(z == g)(lambda: took(three, sem))

    def block(item):
        return item[1] * 2 + core

    def role(item, shift):
        return lax.rem(x + RING - item[1], RING) == shift

    def to_x(k):
        return lax.rem(x + k, RING) * 2 + core

    def l_copy(item, g, dy):
        return pltpu.make_async_remote_copy(src_ref=piece(block(item)), dst_ref=piece(block(item)), send_sem=l_send, recv_sem=l_recv.at[item[0]],
                                            device_id=(0, there(g, dy), col), device_id_type=MESH)

    def spread(g):
        for item in ITEMS:
            pl.when((z == item[0]) & role(item, 0))(lambda item=item: others(g, lambda dy: l_copy(item, g, dy).start(), L_SHIFTS))

    def b_copy(h, g, dy):
        return pltpu.make_async_remote_copy(src_ref=b_own.at[:, cols(there(g, dy), h)], dst_ref=b_all.at[row, :, within(h)], send_sem=b_send,
                                            recv_sem=b_recv.at[h, z], device_id=(0, there(g, dy), col), device_id_type=MESH)

    def b_line(h, k):
        for dy in B_SHIFTS:
            if k or dy:
                b_copy(h, lax.rem(z + k, RING), dy).start()

    for g in range(RING):
        pl.when(g < z)(lambda g=g: spread(g))
    for g in range(RING):
        @pl.when(g == z)
        def _(g=g):
            pl.when(y < RING - 1)(lambda: pl.semaphore_wait(ack.at[g], RING - 1 - y))
            spread(g)
    loads[1].wait()
    for h, k in B_FIRST:
        b_line(h, k)
    for g in range(RING):
        @pl.when(g > z)
        def _(g=g):
            pl.semaphore_wait(ack.at[g], RING)
            spread(g)
    for h, k in B_ORDER:
        b_line(h, k)
    loads[2].wait()

    def s_copy(item, k):
        part = l_all.at[block(item), pl.ds(item[0] * group, group)]
        return pltpu.make_async_remote_copy(src_ref=part, dst_ref=part, send_sem=s_send, recv_sem=s_recv.at[item[0], item[1]],
                                            device_id=(0, row, to_x(k)), device_id_type=MESH)

    def c_copy(item):
        part = l_all.at[block(item), pl.ds(item[0] * group, group)]
        return pltpu.make_async_remote_copy(src_ref=part, dst_ref=part, send_sem=c_send, recv_sem=c_recv.at[item[0]],
                                            device_id=(0, row, partner), device_id_type=MESH)

    def upward(item):
        return jnp.where(core == 0, ITEMS[item][0], ITEMS[item][1]) == 1

    def first(item):
        @pl.when(role(item, 0))
        def _():
            from_line(item[0], l_all.at[0, pl.ds(0, group)], l_all.at[0, pl.ds(0, group - rows)], l_recv.at[item[0]])
            s_copy(item, 1).start()
            s_copy(item, 3).start()
            c_copy(item).start()

    def near(item):
        @pl.when(role(item, 1) | role(item, 3))
        def _():
            s_copy(item, 1).wait_recv()
            pl.when(role(item, 1) & upward(item))(lambda: s_copy(item, 1).start())
            pl.when(role(item, 3) & jnp.logical_not(upward(item)))(lambda: s_copy(item, 3).start())
            c_copy(item).start()

    def far(item):
        @pl.when(role(item, 2))
        def _():
            s_copy(item, 1).wait_recv()
            c_copy(item).start()

    def across(g):
        took(l_all.at[pl.ds(0, g + 1), pl.ds(0, group)], c_recv.at[g])

    def each(act, g):
        for item in ITEMS:
            if item[0] == g:
                act(item)

    pl.when(core == 1)(lambda: pl.semaphore_wait(ack_core, 1))
    for k in range(1, RING):
        pl.when(k > x)(lambda k=k: pl.semaphore_wait(ack_x.at[k], 1))
    def x_copy(h, g, dy):
        return pltpu.make_async_remote_copy(src_ref=x_all.at[there(g, dy), :, within(h)], dst_ref=o_ref.at[:, cols(row, h)], send_sem=x_send,
                                            recv_sem=x_recv, device_id=(0, there(g, dy), col), device_id_type=MESH)

    def finish(h, g):
        from_line(g, b_all.at[pl.ds(0, RING), :, within(h)], b_all.at[pl.ds(0, RING - 1), :, within(h)], b_recv.at[h, g])
        depth, (start, width) = (g + 1) * group, PARTS[h]
        left = jnp.concatenate([l_all[k, g * group:(g + 1) * group, :] for k in range(2 * (g + 1))], axis=1)
        right = b_all[:(g + 1) * RING, :, start:start + width].reshape(depth, width)
        total = jnp.dot(left, right, preferred_element_type=jnp.float32)
        x_all[g * RING:(g + 1) * RING, :, start:start + width] = total.astype(jnp.bfloat16).reshape(RING, rows, width)
        others(g, lambda dy: x_copy(h, g, dy).start(), X_SHIFTS)

    stages = {'first': first, 'near': near, 'far': far}
    for name, *at in SEQUENCE:
        if name == 'across':
            across(*at)
        elif name == 'finish':
            finish(*at)
        else:
            each(stages[name], *at)
    o_ref[:, whole(row)] = x_all[row]

    units = pl.ds(0, group)
    for item in ITEMS:
        pl.when((z == item[0]) & role(item, 0))(lambda: took(l_all.at[0, pl.ds(0, 15 * rows)], l_send))
    for c in (0, 1):
        for v in range(RING):
            count = sent_along_x(c, v)
            assert 1 <= count <= 8
            pl.when((core == c) & (x == v))(lambda count=count: took(l_all.at[pl.ds(0, count), units], s_send))
    took(l_all.at[pl.ds(0, 5), pl.ds(0, 2 * group)], c_send)
    took(b_all.at[pl.ds(0, 15)], b_send)
    took(b_all.at[pl.ds(0, 15)], x_send)
    took(b_all.at[pl.ds(0, 15)], x_recv)


def sent_along_x(c, v):
    count = 0
    for (_, source), up in ITEMS.items():
        count += 2 if source == v else 0
        count += 1 if (v - source) % RING == (1 if up[c] else 3) else 0
    return count


def solution(mesh):
    block_spec = P(('batch', 'row'), 'col')
    dma, vmem, plain = pltpu.SemaphoreType.DMA, pltpu.VMEM, pltpu.SemaphoreType.REGULAR

    def step(l_block, b_block):
        rows, columns = b_block.shape
        return pl.pallas_call(
            kernel,
            out_shape=pltpu.VMEM(b_block.shape, b_block.dtype),
            in_specs=[pl.BlockSpec(memory_space=pl.ANY)] * 2,
            out_specs=pl.BlockSpec(memory_space=pltpu.VMEM),
            scratch_shapes=[
                vmem((rows, columns), jnp.bfloat16),
                vmem((16, rows, columns // 16), jnp.bfloat16),
                vmem((8, 16 * rows, 128), jnp.bfloat16),
                vmem((16, rows, columns // 16), jnp.bfloat16),
                dma((3,)), dma(()), dma((len(PARTS), RING)), dma(()), dma(()), dma(()), dma((RING,)),
                dma(()), dma((RING, RING)), dma(()), dma((RING,)), plain((RING,)), plain((RING,)), plain(()),
            ],
            compiler_params=pltpu.CompilerParams(collective_id=0, has_side_effects=True),
        )(l_block, b_block)

    return jax.shard_map(step, mesh=mesh, in_specs=(block_spec, block_spec), out_specs=block_spec, check_vma=False)
```

time: 140 us -> 37.3 us (0.27)
  waiting for transfers between devices: 103 us -> 0 us
  Pallas kernels: 0 us -> 36.2 us
  between operations: 13.4 us -> 0.01 us
  blocking collectives: 13.2 us -> 0 us
  matrix products: 9.76 us -> 0 us
    all_gather x1 -> x0, waiting for transfers between devices: 102 us -> none  [local_product(): b_strip = lax.all_gather(b_block, 'row', axis=0, tiled=True)]
    pallas_call x0 -> x1, Pallas kernels: none -> 36.2 us  [step(): pl.pallas_call(kernel, out_shape=pltpu.VMEM(b_block.shape, b_block.dtype)...]
    all_gather x1 -> x0, blocking collectives: 13.2 us -> none  [local_product(): l_strip = lax.all_gather(l_block, 'col', axis=1, tiled=True)]
    dot_general x1 -> x0, matrix products: 9.76 us -> none  [local_product(): result = jnp.dot(l_strip, b_strip, preferred_element_type=jnp.float32)]
  transfers between devices with their start and end apart: 1 -> 0, of which waited for: 1 -> 0; matrix products, arithmetic and copies ran while one was open for 0% -> 0% of each run, Pallas kernels for 0% -> 0%
where the time goes in v4:
time: 37.3 us; the launch traced here: 37.1 us
  Pallas kernels  36.2 us (97%)
  local copies, waits for them, and re-layouts  0.97 us (3%)
    pallas_call x1, Pallas kernels, step(): pl.pallas_call(kernel, out_shape=pltpu.VMEM(b_block.shape, b_block.dtype)...  36.2 us
    unnamed x1, local copies, waits for them, and re-layouts  0.97 us

profile of v4, /device:TPU:32, one launch (start us, length us, event | category | flops | bytes accessed | tf_op | source)
XLA Modules:
  0.0 37.1 jit_solution(8896089477930697947)
XLA Ops:
  0.0 36.2 %shard_map.28 = bf16[64,8192]{1,0:T(8,128)(2,1)S(1)} custom-call(bf16[64,128]{1,0:T(8,128)(2,1)} %l_ref.1, bf16[64,8192]{1,0:T(8,128)(2,1)} %b_ref.1), custom_call_target="tpu_custom_call" | custom-call | tf_op jit(solution)/shard_map/pallas_call | solution.py:258
  36.2 1.0 %copy.4 = bf16[64,8192]{1,0:T(8,128)(2,1)} copy(bf16[64,8192]{1,0:T(8,128)(2,1)S(1)} %shard_map.28) | data formatting | bytes 2097152

commit v5 on v4

--- a/solution.py
+++ b/solution.py
@@ -12,22 +12,22 @@
     ('first', 0),
     ('first', 1),
     ('first', 2),
+    ('first', 3),
     ('near', 0),
-    ('first', 3),
     ('near', 1),
+    ('near', 2),
+    ('near', 3),
     ('far', 0),
-    ('near', 2),
     ('across', 0),
+    ('far', 1),
     ('finish', 0, 0),
-    ('far', 1),
-    ('near', 3),
+    ('far', 2),
     ('across', 1),
     ('finish', 0, 1),
-    ('far', 2),
+    ('far', 3),
     ('across', 2),
     ('finish', 0, 2),
     ('finish', 1, 0),
-    ('far', 3),
     ('across', 3),
     ('finish', 0, 3),
     ('finish', 1, 1),
@@ -37,7 +37,7 @@
 B_FIRST = ((0, 0), (1, 0))
 B_ORDER = ((0, 1), (0, 2), (0, 3), (1, 1), (1, 2), (1, 3))
 B_SHIFTS = (1, 3, 2, 0)
-X_SHIFTS = (2, 1, 3, 0)
+X_SHIFTS = (1, 3, 2, 0)
 L_SHIFTS = (1, 3, 2, 0)
 ITEMS = {
     (0, 0): (0, 0),
@@ -160,7 +160,7 @@
 
     def s_copy(item, k):
         part = l_all.at[block(item), pl.ds(item[0] * group, group)]
-        return pltpu.make_async_remote_copy(src_ref=part, dst_ref=part, send_sem=s_send, recv_sem=s_recv.at[item[0], item[1]],
+        return pltpu.make_async_remote_copy(src_ref=part, dst_ref=part, send_sem=s_send, recv_sem=s_recv.at[list(ITEMS).index(item)],
                                             device_id=(0, row, to_x(k)), device_id_type=MESH)
 
     def c_copy(item):
@@ -266,7 +266,7 @@
                 vmem((8, 16 * rows, 128), jnp.bfloat16),
                 vmem((16, rows, columns // 16), jnp.bfloat16),
                 dma((3,)), dma(()), dma((len(PARTS), RING)), dma(()), dma(()), dma(()), dma((RING,)),
-                dma(()), dma((RING, RING)), dma(()), dma((RING,)), plain((RING,)), plain((RING,)), plain(()),
+                dma(()), dma((len(ITEMS),)), dma(()), dma((RING,)), plain((RING,)), plain((RING,)), plain(()),
             ],
             compiler_params=pltpu.CompilerParams(collective_id=0, has_side_effects=True),
         )(l_block, b_block)

time: 37.3 us -> 37.6 us (level)
  no operation moved by 1% of the time
where the time goes in v5:
time: 37.6 us; the launch traced here: 37.4 us
  Pallas kernels  36.4 us (97%)
  local copies, waits for them, and re-layouts  0.97 us (3%)
    pallas_call x1, Pallas kernels, step(): pl.pallas_call(kernel, out_shape=pltpu.VMEM(b_block.shape, b_block.dtype)...  36.4 us
    unnamed x1, local copies, waits for them, and re-layouts  0.97 us

profile of v5, /device:TPU:32, one launch (start us, length us, event | category | flops | bytes accessed | tf_op | source)
XLA Modules:
  0.0 37.4 jit_solution(14677891939750269118)
XLA Ops:
  0.0 36.4 %shard_map.28 = bf16[64,8192]{1,0:T(8,128)(2,1)S(1)} custom-call(bf16[64,128]{1,0:T(8,128)(2,1)} %l_ref.1, bf16[64,8192]{1,0:T(8,128)(2,1)} %b_ref.1), custom_call_target="tpu_custom_call" | custom-call | tf_op jit(solution)/shard_map/pallas_call | solution.py:258
  36.4 1.0 %copy.4 = bf16[64,8192]{1,0:T(8,128)(2,1)} copy(bf16[64,8192]{1,0:T(8,128)(2,1)S(1)} %shard_map.28) | data formatting | bytes 2097152

commit v6 on v4

--- a/solution.py
+++ b/solution.py
@@ -160,7 +160,7 @@
 
     def s_copy(item, k):
         part = l_all.at[block(item), pl.ds(item[0] * group, group)]
-        return pltpu.make_async_remote_copy(src_ref=part, dst_ref=part, send_sem=s_send, recv_sem=s_recv.at[item[0], item[1]],
+        return pltpu.make_async_remote_copy(src_ref=part, dst_ref=part, send_sem=s_send, recv_sem=s_recv.at[list(ITEMS).index(item)],
                                             device_id=(0, row, to_x(k)), device_id_type=MESH)
 
     def c_copy(item):
@@ -266,7 +266,7 @@
                 vmem((8, 16 * rows, 128), jnp.bfloat16),
                 vmem((16, rows, columns // 16), jnp.bfloat16),
                 dma((3,)), dma(()), dma((len(PARTS), RING)), dma(()), dma(()), dma(()), dma((RING,)),
-                dma(()), dma((RING, RING)), dma(()), dma((RING,)), plain((RING,)), plain((RING,)), plain(()),
+                dma(()), dma((len(ITEMS),)), dma(()), dma((RING,)), plain((RING,)), plain((RING,)), plain(()),
             ],
             compiler_params=pltpu.CompilerParams(collective_id=0, has_side_effects=True),
         )(l_block, b_block)

time: 37.3 us -> 37.2 us (level)
  no operation moved by 1% of the time
where the time goes in v6:
time: 37.2 us; the launch traced here: 37.1 us
  Pallas kernels  36.1 us (97%)
  local copies, waits for them, and re-layouts  0.97 us (3%)
    pallas_call x1, Pallas kernels, step(): pl.pallas_call(kernel, out_shape=pltpu.VMEM(b_block.shape, b_block.dtype)...  36.1 us
    unnamed x1, local copies, waits for them, and re-layouts  0.97 us

profile of v6, /device:TPU:32, one launch (start us, length us, event | category | flops | bytes accessed | tf_op | source)
XLA Modules:
  0.0 37.1 jit_solution(11096555201071010236)
XLA Ops:
  0.0 36.1 %shard_map.28 = bf16[64,8192]{1,0:T(8,128)(2,1)S(1)} custom-call(bf16[64,128]{1,0:T(8,128)(2,1)} %l_ref.1, bf16[64,8192]{1,0:T(8,128)(2,1)} %b_ref.1), custom_call_target="tpu_custom_call" | custom-call | tf_op jit(solution)/shard_map/pallas_call | solution.py:258
  36.1 1.0 %copy.4 = bf16[64,8192]{1,0:T(8,128)(2,1)} copy(bf16[64,8192]{1,0:T(8,128)(2,1)S(1)} %shard_map.28) | data formatting | bytes 2097152

commit v7 on v6

--- a/solution.py
+++ b/solution.py
@@ -53,7 +53,7 @@
 }
 
 
-def kernel(l_ref, b_ref, o_ref, b_own, b_all, l_all, x_all, load_sem, b_send, b_recv, x_send, x_recv, l_send, l_recv, s_send,
+def kernel(l_ref, b_ref, o_ref, b_own, b_all, l_all, x_all, load_sem, b_send, b_recv, x_recv, l_send, l_recv, s_send,
            s_recv, c_send, c_recv, ack, ack_x, ack_core):
     row, col = lax.axis_index('row'), lax.axis_index('col')
     z, y, x, core = row // RING, row % RING, col // 2, col % 2
@@ -205,7 +205,7 @@
     for k in range(1, RING):
         pl.when(k > x)(lambda k=k: pl.semaphore_wait(ack_x.at[k], 1))
     def x_copy(h, g, dy):
-        return pltpu.make_async_remote_copy(src_ref=x_all.at[there(g, dy), :, within(h)], dst_ref=o_ref.at[:, cols(row, h)], send_sem=x_send,
+        return pltpu.make_async_remote_copy(src_ref=x_all.at[there(g, dy), :, within(h)], dst_ref=o_ref.at[:, cols(row, h)], send_sem=b_send,
                                             recv_sem=x_recv, device_id=(0, there(g, dy), col), device_id_type=MESH)
 
     def finish(h, g):
@@ -236,8 +236,7 @@
             assert 1 <= count <= 8
             pl.when((core == c) & (x == v))(lambda count=count: took(l_all.at[pl.ds(0, count), units], s_send))
     took(l_all.at[pl.ds(0, 5), pl.ds(0, 2 * group)], c_send)
-    took(b_all.at[pl.ds(0, 15)], b_send)
-    took(b_all.at[pl.ds(0, 15)], x_send)
+    took(l_all.at[:, pl.ds(0, 15 * rows)], b_send)
     took(b_all.at[pl.ds(0, 15)], x_recv)
 
 
@@ -265,7 +264,7 @@
                 vmem((16, rows, columns // 16), jnp.bfloat16),
                 vmem((8, 16 * rows, 128), jnp.bfloat16),
                 vmem((16, rows, columns // 16), jnp.bfloat16),
-                dma((3,)), dma(()), dma((len(PARTS), RING)), dma(()), dma(()), dma(()), dma((RING,)),
+                dma((3,)), dma(()), dma((len(PARTS), RING)), dma(()), dma(()), dma((RING,)),
                 dma(()), dma((len(ITEMS),)), dma(()), dma((RING,)), plain((RING,)), plain((RING,)), plain(()),
             ],
             compiler_params=pltpu.CompilerParams(collective_id=0, has_side_effects=True),

time: 37.2 us -> 37.2 us (level)
  no operation moved by 1% of the time
where the time goes in v7:
time: 37.2 us; the launch traced here: 37.1 us
  Pallas kernels  36.1 us (97%)
  local copies, waits for them, and re-layouts  0.97 us (3%)
    pallas_call x1, Pallas kernels, step(): pl.pallas_call(kernel, out_shape=pltpu.VMEM(b_block.shape, b_block.dtype)...  36.1 us
    unnamed x1, local copies, waits for them, and re-layouts  0.97 us

profile of v7, /device:TPU:32, one launch (start us, length us, event | category | flops | bytes accessed | tf_op | source)
XLA Modules:
  0.0 37.1 jit_solution(3215358146050768168)
XLA Ops:
  0.0 36.1 %shard_map.28 = bf16[64,8192]{1,0:T(8,128)(2,1)S(1)} custom-call(bf16[64,128]{1,0:T(8,128)(2,1)} %l_ref.1, bf16[64,8192]{1,0:T(8,128)(2,1)} %b_ref.1), custom_call_target="tpu_custom_call" | custom-call | tf_op jit(solution)/shard_map/pallas_call | solution.py:257
  36.1 1.0 %copy.4 = bf16[64,8192]{1,0:T(8,128)(2,1)} copy(bf16[64,8192]{1,0:T(8,128)(2,1)S(1)} %shard_map.28) | data formatting | bytes 2097152

commit v8 on v7

--- a/solution.py
+++ b/solution.py
@@ -102,7 +102,7 @@
     for r in range(RING * RING - 1):
         pl.when(r < row)(lambda r=r: greet(ack.at[z], r, col))
     for k in range(RING - 1):
-        pl.when(k < x)(lambda k=k: greet(ack_x.at[x], row, k * 2 + core))
+        pl.when(k < x)(lambda k=k: greet(ack_x.at[x - 1], row, k * 2 + core))
     pl.when(core == 0)(lambda: greet(ack_core, row, partner))
     loads[0].wait()
 
@@ -203,7 +203,7 @@
 
     pl.when(core == 1)(lambda: pl.semaphore_wait(ack_core, 1))
     for k in range(1, RING):
-        pl.when(k > x)(lambda k=k: pl.semaphore_wait(ack_x.at[k], 1))
+        pl.when(k > x)(lambda k=k: pl.semaphore_wait(ack_x.at[k - 1], 1))
     def x_copy(h, g, dy):
         return pltpu.make_async_remote_copy(src_ref=x_all.at[there(g, dy), :, within(h)], dst_ref=o_ref.at[:, cols(row, h)], send_sem=b_send,
                                             recv_sem=x_recv, device_id=(0, there(g, dy), col), device_id_type=MESH)
@@ -265,7 +265,7 @@
                 vmem((8, 16 * rows, 128), jnp.bfloat16),
                 vmem((16, rows, columns // 16), jnp.bfloat16),
                 dma((3,)), dma(()), dma((len(PARTS), RING)), dma(()), dma(()), dma((RING,)),
-                dma(()), dma((len(ITEMS),)), dma(()), dma((RING,)), plain((RING,)), plain((RING,)), plain(()),
+                dma(()), dma((len(ITEMS),)), dma(()), dma((RING,)), plain((RING,)), plain((RING - 1,)), plain(()),
             ],
             compiler_params=pltpu.CompilerParams(collective_id=0, has_side_effects=True),
         )(l_block, b_block)

time: 37.2 us -> 37.2 us (level)
  no operation moved by 1% of the time
where the time goes in v8:
time: 37.2 us; the launch traced here: 37.1 us
  Pallas kernels  36.1 us (97%)
  local copies, waits for them, and re-layouts  0.97 us (3%)
    pallas_call x1, Pallas kernels, step(): pl.pallas_call(kernel, out_shape=pltpu.VMEM(b_block.shape, b_block.dtype)...  36.1 us
    unnamed x1, local copies, waits for them, and re-layouts  0.97 us

profile of v8, /device:TPU:32, one launch (start us, length us, event | category | flops | bytes accessed | tf_op | source)
XLA Modules:
  0.0 37.1 jit_solution(246416284298244042)
XLA Ops:
  0.0 36.1 %shard_map.28 = bf16[64,8192]{1,0:T(8,128)(2,1)S(1)} custom-call(bf16[64,128]{1,0:T(8,128)(2,1)} %l_ref.1, bf16[64,8192]{1,0:T(8,128)(2,1)} %b_ref.1), custom_call_target="tpu_custom_call" | custom-call | tf_op jit(solution)/shard_map/pallas_call | solution.py:257
  36.1 1.0 %copy.4 = bf16[64,8192]{1,0:T(8,128)(2,1)} copy(bf16[64,8192]{1,0:T(8,128)(2,1)S(1)} %shard_map.28) | data formatting | bytes 2097152
